TPU v7x, 32 devices: a whole 2x2x4 slice. The times are simulated.
32 devices in a mesh: seq: 16 (over z, x, core), head: 2 (over y).
Axes of the slice: x: 2, y: 2, z: 4, core: 2. Of those that a mesh axis runs over, the one named last changes fastest.
Arguments:
- query: bfloat16 [8192, 1024], P('seq', 'head'), may hold values from -6 to 6
- key_rows: bfloat16 [8192, 128], P('seq'), may hold values from -6 to 6
- value_rows: bfloat16 [8192, 128], P('seq'), may hold values from -6 to 6
- output: bfloat16 [8192, 1024], P('seq', 'head'), may hold values from -1.5 to 1.5
- grad_output: bfloat16 [8192, 1024], P('seq', 'head'), may hold values from -144 to 144
- log_norm: float32 [8, 8192], P('head', 'seq'), may hold values from 0.5 to 12
- stripe: int32 [16], replicated, may hold values from 0 to 15, each once
Outputs:
- grad_query: bfloat16 [8192, 1024], P('seq', 'head')
- grad_key: bfloat16 [8192, 128], P(('seq', 'head'))
- grad_value: bfloat16 [8192, 128], P(('seq', 'head'))
Inputs may be any that keep to these rules, and one draw needn't show every extreme that they name: stripe is a permutation of 0 to 15.
All inputs are finite; a program needn't handle non-finite values.
Results may differ from a plain program's by a relative error of at most 0.0051.
Values may be sent and summed in bfloat16 or wider, within the bound.
A program may use at most 192 MiB of HBM per device.

v0:
```python
import functools

import jax
import jax.numpy as jnp
from jax import lax
from jax.experimental import pallas as pl
from jax.experimental.pallas import tpu as pltpu
from jax.sharding import PartitionSpec as P

WINDOW = 8
GROUP = WINDOW // 2
LOG2E = 1.4426950408889634
F32 = jnp.float32
BF16 = jnp.bfloat16
STEPS = ((0, 0), (1, 1), (1, 0), (1, 3), (1, 2), (0, 3), (0, 2), (0, 1))
GIVEN = {(1, 1): 0, (1, 3): 1, (0, 3): 2}
TAKEN = {(1, 0): 0, (1, 2): 1, (0, 2): 2}
SENT = ((0, 0), (1, 0), (1, 2), (0, 2), (0, 1))


def dot(a, b, ca, cb):
    return lax.dot_general(a, b, (((ca,), (cb,)), ((), ())), preferred_element_type=F32)


def kernel(
    n, stripe, q_hbm, k_hbm, v_hbm, o_hbm, g_hbm, lse_hbm,
    dq_out, dk_out, dv_out,
    q, g, o, lse, delta, kv, dqt, acc, give, take, part, rx, zs, fin,
    in_sem, kv_send, kv_recv, d_send, d_recv, p_send, p_recv, z_send, z_recv,
):
    me = lax.axis_index("seq")
    y = lax.axis_index("head")
    j = lax.rem(me, GROUP)
    base = me - j
    S, D2 = kv.shape[1:]
    D = D2 // 2
    H = q.shape[1] // D
    half = S // 2
    factor = D ** -0.5

    def mate(t):
        low = j % 2
        high = j // 2
        low = (1 - low) if t & 1 else low
        high = (1 - high) if t & 2 else high
        return high * 2 + low

    def at(t):
        return base + mate(t)

    def plane(d):
        return lax.rem(me + d * GROUP + n, n)

    loads = [
        pltpu.make_async_copy(k_hbm, kv.at[j, :, pl.ds(0, D)], in_sem.at[0]),
        pltpu.make_async_copy(v_hbm, kv.at[j, :, pl.ds(D, D)], in_sem.at[1]),
        pltpu.make_async_copy(q_hbm, q, in_sem.at[2]),
        pltpu.make_async_copy(g_hbm, g, in_sem.at[3]),
        pltpu.make_async_copy(o_hbm, o, in_sem.at[4]),
        pltpu.make_async_copy(lse_hbm, lse, in_sem.at[5]),
    ]
    for c in loads:
        c.start()

    barrier = pltpu.get_barrier_semaphore()
    peers = [(at(t), y) for t in (1, 2, 3)] + [(at(t), 1 - y) for t in range(4)]
    peers += [(plane(d), y) for d in (1, -1, 2, -2)]
    for p in peers:
        pl.semaphore_signal(barrier, inc=1, device_id=p, device_id_type=pl.DeviceIdType.MESH)
    loads[0].wait()
    loads[1].wait()
    pl.semaphore_wait(barrier, len(peers))

    A = lambda i: i
    B = lambda i: GROUP + i
    C = 2 * GROUP

    def remote(src, dst, ss, rs, to):
        return pltpu.make_async_remote_copy(
            src_ref=src, dst_ref=dst, send_sem=ss, recv_sem=rs,
            device_id=to, device_id_type=pl.DeviceIdType.MESH,
        )

    def kv_copy(src, dst, sem, to):
        return remote(kv.at[src], kv.at[dst], kv_send.at[sem], kv_recv.at[dst], (to, y))

    up_b = kv_copy(A(j), B(j), 0, plane(1))
    up_c = kv_copy(B(j), C, 1, plane(1))
    own = {t: kv_copy(A(j), A(j), 1 + t, at(t)) for t in (1, 2)}
    late = {t: kv_copy(C, A(j), 1 + t, at(t)) for t in (1, 2)}
    b_out = {t: kv_copy(B(j), B(j), 3 + t, at(t)) for t in (1, 2)}
    b_relay = kv_copy(B(mate(2)), B(mate(2)), 6, at(1))
    a_relay = kv_copy(A(mate(2)), A(mate(2)), 7, at(1))

    def kv_arrived(slot):
        kv_copy(slot, slot, 0, at(1)).wait_recv()

    up_b.start()
    for t in (1, 2):
        pl.when(mate(t) > j)(own[t].start)

    for c in loads[2:]:
        c.wait()

    ones = jnp.ones((8, D), BF16)
    for h in range(H):
        cols = slice(h * D, (h + 1) * D)
        prod = g[:, cols].astype(F32) * o[:, cols].astype(F32)
        hi = prod.astype(BF16)
        rest = prod - hi.astype(F32)
        mid = rest.astype(BF16)
        low = (rest - mid.astype(F32)).astype(BF16)
        total = dot(ones, hi, 1, 1) + dot(ones, mid, 1, 1) + dot(ones, low, 1, 1)
        delta[h] = total * factor
    dqt[...] = jnp.zeros_like(dqt)
    own_stripe = stripe[me]

    rows = lax.broadcasted_iota(jnp.int32, (half, half), 0)
    diff = lax.broadcasted_iota(jnp.int32, (half, half), 1) - rows

    def heads(slot, least, first):
        def one(h):
            cols = pl.ds(pl.multiple_of(h * D, D), D)
            k0, k1 = kv[slot, :half, :D], kv[slot, half:, :D]
            v0, v1 = kv[slot, :half, D:], kv[slot, half:, D:]
            qh, gh = q[:, cols], g[:, cols]
            l2 = lse[pl.ds(h, 1), :] * LOG2E
            dl = delta[h, 0:1, :]
            s0 = dot(k0, qh, 1, 1)
            s1 = dot(k1, qh[half:], 1, 1)
            w0 = dot(v0, gh, 1, 1)
            w1 = dot(v1, gh[half:], 1, 1)
            p0 = jnp.exp2(s0 * (factor * LOG2E) - l2)
            open_ = diff >= least
            p0 = jnp.concatenate([jnp.where(open_, p0[:, :half], 0.0), p0[:, half:]], axis=1)
            p1 = jnp.where(open_, jnp.exp2(s1 * (factor * LOG2E) - l2[:, half:]), 0.0)
            d0 = (p0 * (w0 * factor - dl)).astype(BF16)
            d1 = (p1 * (w1 * factor - dl[:, half:])).astype(BF16)
            dv0 = dot(p0.astype(BF16), gh, 1, 0)
            dv1 = dot(p1.astype(BF16), gh[half:], 1, 0)
            dk0 = dot(d0, qh, 1, 0)
            dk1 = dot(d1, qh[half:], 1, 0)
            dqt[h, :, :] += dot(k0, d0, 0, 0)
            dqt[h, :, half:] += dot(k1, d1, 0, 0)
            return dk0, dv0, dk1, dv1

        return one

    def compute(slot, late_flag, i, between):
        if late_flag:
            source = base - GROUP + i
        else:
            source = base + i - jnp.where(i > j, 2 * GROUP, 0)
        source = lax.rem(source + n, n)
        least = jnp.where(stripe[source] <= own_stripe, 0, 1)
        one = heads(slot, least, True)

        def pair(h0, keep):
            a = one(h0)
            b = one(h0 + 1)
            for m in range(4):
                r, c = m // 2, m % 2
                s = a[m] + b[m]
                if keep:
                    s = s + acc[r, :, c * D:(c + 1) * D]
                acc[r, :, c * D:(c + 1) * D] = s

        pair(0, False)
        between()

        @pl.loop(1, H // 2)
        def _(m):
            pair(2 * m, True)

    def part_copies(key):
        late_flag, t = key
        to = at(t)
        slot = SENT.index(key)
        res = []
        if t:
            res.append(remote(part.at[slot, y], rx.at[slot, 0],
                              p_send.at[slot, 0], p_recv.at[slot, 0], (to, y)))
        res.append(remote(part.at[slot, 1 - y], rx.at[slot, 1],
                          p_send.at[slot, 1], p_recv.at[slot, 1], (to, 1 - y)))
        return res

    def pair_copy(m):
        return remote(give.at[m], take.at[m], d_send.at[m], d_recv.at[m], (at(1), y))

    def send_part(key):
        if key in GIVEN:
            pair_copy(GIVEN[key]).start()
        else:
            for c in part_copies(key):
                c.start()

    z_copies = [
        remote(zs.at[m], fin.at[m], z_send.at[m], z_recv.at[m], (plane(-1 - m), y)) for m in range(2)
    ]

    def arrived_part(flag, t):
        slot = SENT.index((flag, t))

        def get(m):
            remote(rx.at[slot, m], rx.at[slot, m], p_send.at[0, 0], p_recv.at[slot, m],
                   (at(1), y)).wait_recv()
            return rx[slot, m].astype(F32)

        first = part[slot, y].astype(F32) if t == 0 else get(0)
        return first + get(1)

    for step, (flag, t) in enumerate(STEPS):
        i = mate(t)
        slot = B(i) if flag else A(i)
        if (flag, t) == (1, 1):
            kv_arrived(B(j))
            up_c.start()
            b_out[1].start()
            b_out[2].start()
            kv_arrived(slot)
        elif (flag, t) == (1, 3):
            kv_arrived(B(mate(2)))
            b_relay.start()
            kv_arrived(C)
            for u in (1, 2):
                pl.when(mate(u) < j)(late[u].start)
            kv_arrived(slot)
        elif (flag, t) == (0, 3):
            kv_arrived(A(mate(2)))
            a_relay.start()
            kv_arrived(slot)
        elif (flag, t) == (0, 1):
            kv_arrived(slot)

        def between():
            if step:
                send_part(STEPS[step - 1])
            if step == 7:
                z_copies[0].start()

        compute(slot, flag, i, between)
        key = (flag, t)
        if key in GIVEN:
            give[GIVEN[key]] = acc[...]
        elif key in TAKEN:
            m = TAKEN[key]
            pair_copy(m).wait_recv()
            part[SENT.index(key)] = (acc[...] + take[m]).astype(BF16)
        else:
            part[SENT.index(key)] = acc[...].astype(BF16)
        if step == 6:
            zs[0] = (arrived_part(1, 0) + arrived_part(1, 2)).astype(BF16)

    send_part(STEPS[-1])

    for h in range(H):
        dq_out[:, h * D:(h + 1) * D] = dqt[h].T.astype(BF16)

    mine = arrived_part(0, 0)
    other = jnp.zeros_like(mine)
    for u in (2, 1):
        x = arrived_part(0, u)
        here = mate(u) > j
        mine = mine + jnp.where(here, x, 0.0)
        other = other + jnp.where(here, 0.0, x)
    zs[1] = other.astype(BF16)
    z_copies[1].start()
    z_copies[0].wait_recv()
    mine = mine + fin[0].astype(F32)
    z_copies[1].wait_recv()
    mine = mine + fin[1].astype(F32)
    dk_out[...] = mine[:, :D].astype(BF16)
    dv_out[...] = mine[:, D:].astype(BF16)

    for c in [up_b, up_c, own[1], own[2], b_out[1], b_out[2], b_relay, a_relay]:
        c.wait_send()
    for key in SENT:
        for c in part_copies(key):
            c.wait_send()
    for m in range(len(GIVEN)):
        pair_copy(m).wait_send()
    for c in z_copies:
        c.wait_send()


def shards(n, query, key_rows, value_rows, output, grad_output, log_norm, stripe):
    S, W = query.shape
    D = key_rows.shape[1]
    H = W // D
    half = S // 2
    any_ = pl.BlockSpec(memory_space=pl.ANY)
    vm = pl.BlockSpec(memory_space=pltpu.VMEM)
    dma = pltpu.SemaphoreType.DMA
    return pl.pallas_call(
        functools.partial(kernel, n),
        out_shape=(
            jax.ShapeDtypeStruct((S, W), BF16),
            jax.ShapeDtypeStruct((half, D), BF16),
            jax.ShapeDtypeStruct((half, D), BF16),
        ),
        in_specs=[pl.BlockSpec(memory_space=pltpu.SMEM)] + [any_] * 6,
        out_specs=(vm, vm, vm),
        scratch_shapes=[
            pltpu.VMEM((S, W), BF16),
            pltpu.VMEM((S, W), BF16),
            pltpu.VMEM((S, W), BF16),
            pltpu.VMEM((H, S), F32),
            pltpu.VMEM((H, 8, S), F32),
            pltpu.VMEM((2 * GROUP + 1, S, 2 * D), BF16),
            pltpu.VMEM((H, D, S), F32),
            pltpu.VMEM((2, half, 2 * D), F32),
            pltpu.VMEM((len(GIVEN), 2, half, 2 * D), F32),
            pltpu.VMEM((len(GIVEN), 2, half, 2 * D), F32),
            pltpu.VMEM((len(SENT), 2, half, 2 * D), BF16),
            pltpu.VMEM((len(SENT), 2, half, 2 * D), BF16),
            pltpu.VMEM((2, half, 2 * D), BF16),
            pltpu.VMEM((2, half, 2 * D), BF16),
            dma((6,)),
            dma((8,)),
            dma((2 * GROUP + 1,)),
            dma((len(GIVEN),)),
            dma((len(GIVEN),)),
            dma((len(SENT), 2)),
            dma((len(SENT), 2)),
            dma((2,)),
            dma((2,)),
        ],
        compiler_params=pltpu.CompilerParams(
            collective_id=0, has_side_effects=True, vmem_limit_bytes=67043328
        ),
        name="window_backward",
    )(stripe, query, key_rows, value_rows, output, grad_output, log_norm)


def solution(mesh):
    placed = (
        P("seq", "head"),
        P("seq", None),
        P("seq", None),
        P("seq", "head"),
        P("seq", "head"),
        P("head", "seq"),
        P(),
    )
    return jax.shard_map(
        functools.partial(shards, mesh.shape["seq"]),
        mesh=mesh,
        in_specs=placed,
        out_specs=(P("seq", "head"), P(("seq", "head"), None), P(("seq", "head"), None)),
        check_vma=False,
    )
```

profile of v0, /device:TPU:0, one launch (start us, length us, event | category | flops | bytes accessed | tf_op | source)
XLA Modules:
  0.0 60.5 jit_solution(668714728883872105)
XLA Ops:
  0.6 56.5 %window_backward.1 = (bf16[512,512]{1,0:T(8,128)(2,1)}, bf16[256,128]{1,0:T(8,128)(2,1)}, bf16[256,128]{1,0:T(8,128)(2,1)}) custom-call(s32[16]{0:T(128)} %stripe.1, bf16[512,512]{1,0:T(8,128)(2,1)} %q_hbm.1, bf16[512,128]{1,0:T(8,128)(2,1)} %k_hbm.1, bf16[512,128]{1,0:T(8,128)(2,1)} %v_hbm.1, bf16[512,512]{1,0:T(8,128)(2,1)} %o_hbm.1, ...), custom_call_target="tpu_custom_call" | custom-call | tf_op jit(solution)/shard_map/window_backward/pallas_call | solution.py:294
  57.1 0.0 copy-start.1
  57.1 1.9 %copy.13 = bf16[512,512]{1,0:T(8,128)(2,1)} copy(bf16[512,512]{1,0:T(8,128)(2,1)} %get-tuple-element.6) | data formatting | bytes 1048576
  59.0 0.0 copy-done.1
  59.0 0.0 copy-start
  59.0 0.6 %copy.14 = bf16[256,128]{1,0:T(8,128)(2,1)} copy(bf16[256,128]{1,0:T(8,128)(2,1)S(1)} %copy-done.1) | data formatting | bytes 131072
  59.7 0.2 copy-done
  59.9 0.6 %copy.15 = bf16[256,128]{1,0:T(8,128)(2,1)} copy(bf16[256,128]{1,0:T(8,128)(2,1)S(1)} %copy-done) | data formatting | bytes 131072
Async XLA Ops:
  57.1 1.9 %copy-start.1 = (bf16[256,128]{1,0:T(8,128)(2,1)S(1)}, bf16[256,128]{1,0:T(8,128)(2,1)}, u32[]{:S(2)}) copy-start(bf16[256,128]{1,0:T(8,128)(2,1)} %get-tuple-element.7) | copy-start | bytes 196612
  59.0 0.9 %copy-start = (bf16[256,128]{1,0:T(8,128)(2,1)S(1)}, bf16[256,128]{1,0:T(8,128)(2,1)}, u32[]{:S(2)}) copy-start(bf16[256,128]{1,0:T(8,128)(2,1)} %get-tuple-element.8) | copy-start | bytes 196612
where the time goes:
time: 60.7 us; the launch traced here: 60.5 us
  Pallas kernels  56.5 us (93%)
  local copies, waits for them, and re-layouts  3.4 us (6%)
  between operations  0.65 us (1%)
    pallas_call x1, Pallas kernels, shards(): pl.pallas_call(functools.partial(kernel, n), out_shape=(jax.ShapeDtypeStr...  56.5 us
    unnamed x7, local copies, waits for them, and re-layouts  3.4 us

commit v1 on v0

v1 whole, which is shorter than its diff:
```python
import functools

import jax
import jax.numpy as jnp
from jax import lax
from jax.experimental import pallas as pl
from jax.experimental.pallas import tpu as pltpu
from jax.sharding import PartitionSpec as P

WINDOW = 8
GROUP = WINDOW // 2
LOG2E = 1.4426950408889634
F32 = jnp.float32
BF16 = jnp.bfloat16
OWN, NEAR, SIDE, FAR, MATE = range(5)
PAIRS = 3
QUADS = ((1, 1), (1, 0), (0, 0))
LAG = 3


def dot(a, b, ca, cb):
    return lax.dot_general(a, b, (((ca,), (cb,)), ((), ())), preferred_element_type=F32)


def kernel(
    n, stripe, q_hbm, k_hbm, v_hbm, o_hbm, g_hbm, lse_hbm,
    dq_out, dk_out, dv_out,
    q, g, o, lse, delta, level, qt, gt, kv, dqt, acc, take, part, rx, zs, fin, dq,
    in_sem, out_sem, kv_send, kv_recv, d_send, d_recv, p_send, p_recv, z_send, z_recv,
):
    me = lax.axis_index("seq")
    y = lax.axis_index("head")
    j = lax.rem(me, GROUP)
    base = me - j
    S, D2 = kv.shape[1:]
    D = D2 // 2
    H = q.shape[1] // D
    half = S // 2
    c = j % 2
    x = j // 2
    factor = D ** -0.5

    def mate(t):
        low = j % 2
        high = j // 2
        low = (1 - low) if t & 1 else low
        high = (1 - high) if t & 2 else high
        return high * 2 + low

    def at(t):
        return base + mate(t)

    def plane(d):
        return lax.rem(me + d * GROUP + n, n)

    loads = [
        pltpu.make_async_copy(k_hbm, kv.at[j, :, pl.ds(0, D)], in_sem.at[0]),
        pltpu.make_async_copy(v_hbm, kv.at[j, :, pl.ds(D, D)], in_sem.at[1]),
        pltpu.make_async_copy(q_hbm, q, in_sem.at[2]),
        pltpu.make_async_copy(g_hbm, g, in_sem.at[3]),
        pltpu.make_async_copy(o_hbm, o, in_sem.at[4]),
        pltpu.make_async_copy(lse_hbm, lse, in_sem.at[5]),
    ]
    for load in loads:
        load.start()

    def owner(t):
        i = mate(t)
        return lax.rem(base + i - jnp.where(i > j, 2 * GROUP, 0) + n, n)

    def partner(t):
        i = mate(t)
        return lax.rem(base + i + jnp.where(i > j, -2 * GROUP, 2 * GROUP) + n, n)

    barrier = pltpu.get_barrier_semaphore()
    peers = [(at(t), y) for t in (1, 2)] + [(at(t), 1 - y) for t in (0, 1, 2)]
    peers += [(plane(d), y) for d in (1, -1)]
    peers += [(partner(t), y) for t in (1, 2)]
    for p in peers:
        pl.semaphore_signal(barrier, inc=1, device_id=p, device_id_type=pl.DeviceIdType.MESH)
    for load in loads:
        load.wait()

    for h in range(H):
        cols = slice(h * D, (h + 1) * D)
        prod = g[:, cols].astype(F32) * o[:, cols].astype(F32)
        total = jnp.sum(prod, axis=1, keepdims=True) * factor
        delta[h] = jnp.broadcast_to(total, (S, D))
        line = jnp.broadcast_to(lse[h:h + 1, :] * LOG2E, (D, S))
        level[h] = line.T
        qt[h] = q[:, cols].T
        gt[h] = g[:, cols].T
    pl.semaphore_wait(barrier, len(peers))

    A = lambda i: i
    B = lambda i: GROUP + i
    C = 2 * GROUP

    def remote(src, dst, ss, rs, to):
        return pltpu.make_async_remote_copy(
            src_ref=src, dst_ref=dst, send_sem=ss, recv_sem=rs,
            device_id=to, device_id_type=pl.DeviceIdType.MESH,
        )

    def kv_copy(src, dst, sem, to):
        return remote(kv.at[src], kv.at[dst], kv_send.at[sem], kv_recv.at[dst], (to, y))

    up_b = kv_copy(A(j), B(j), 0, plane(1))
    up_c = kv_copy(B(j), C, 1, plane(1))
    own = {t: kv_copy(A(j), A(j), 1 + t, at(t)) for t in (1, 2)}
    late = {t: kv_copy(C, A(j), 1 + t, at(t)) for t in (1, 2)}
    b_out = {t: kv_copy(B(j), B(j), 3 + t, at(t)) for t in (1, 2)}
    b_relay = kv_copy(B(mate(2)), B(mate(2)), 6, at(1))
    a_relay = kv_copy(A(mate(2)), A(mate(2)), 7, at(1))

    def kv_arrived(slot):
        kv_copy(slot, slot, 0, at(1)).wait_recv()

    def on(core, *acts):
        @pl.when(c == core)
        def _():
            for act in acts:
                act()

    def spread_b():
        kv_arrived(B(j))
        b_out[1].start()
        b_out[2].start()
        pl.when(j > 0)(up_c.start)

    def relay_b():
        kv_arrived(B(mate(2)))
        b_relay.start()

    def relay_a():
        kv_arrived(A(mate(2)))
        a_relay.start()

    def pass_c():
        @pl.when(j > 0)
        def _():
            kv_arrived(C)
            pl.when(x == 1)(late[2].start)
            pl.when(c == 1)(late[1].start)

    def side_own():
        pl.when(x == 0)(own[2].start)

    on(1, up_b.start)
    on(0, own[1].start, side_own)

    dqt[...] = jnp.zeros_like(dqt)
    own_stripe = stripe[me]

    cols_ = lax.broadcasted_iota(jnp.int32, (half, half), 1)
    diff = lax.broadcasted_iota(jnp.int32, (half, half), 0) - cols_

    def rows(i):
        return slice(i * half, (i + 1) * half)

    def wide(a):
        return jnp.concatenate([a] * (half // D), axis=1)

    def pair(slot, least, k, h0):
        units = [(h, r, w) for h in (h0, h0 + 1) for r, w in QUADS]
        open_ = diff >= least
        ks = [kv[slot, rows(w), :D] for w in range(2)]
        vs = [kv[slot, rows(w), D:] for w in range(2)]
        dk, dv, dq_part = {}, {}, {}

        def products(unit):
            h, r, w = unit
            cols = slice(h * D, (h + 1) * D)
            return dot(q[rows(r), cols], ks[w], 1, 1), dot(g[rows(r), cols], vs[w], 1, 1)

        def add(sums, key, term):
            sums[key] = sums[key] + term if key in sums else term

        def use(unit, score, weight):
            h, r, w = unit
            p = jnp.exp2(score * (factor * LOG2E) - wide(level[h, rows(r)]))
            if r == w:
                p = jnp.where(open_, p, 0.0)
            d = (p * (weight * factor - wide(delta[h, rows(r)]))).astype(BF16)
            add(dv, w, dot(gt[h, :, rows(r)], p.astype(BF16), 1, 0))
            add(dk, w, dot(qt[h, :, rows(r)], d, 1, 0))
            add(dq_part, (h, r), dot(d, ks[w], 1, 0))
            if w == 0:
                dqt[h, rows(r)] += dq_part[h, r]

        waiting = []
        for unit in units:
            waiting.append((unit, products(unit)))
            if len(waiting) > LAG:
                unit, found = waiting.pop(0)
                use(unit, *found)
        for unit, found in waiting:
            use(unit, *found)
        for w in range(2):
            for m, total in enumerate((dk[w], dv[w])):
                if h0:
                    total = total + acc[k, w, m * D:(m + 1) * D, :]
                acc[k, w, m * D:(m + 1) * D, :] = total

    def compute(slot, late_flag, i, k, between):
        if late_flag:
            source = base - GROUP + i
        else:
            source = base + i - jnp.where(i > j, 2 * GROUP, 0)
        source = lax.rem(source + n, n)
        least = jnp.where(stripe[source] <= own_stripe, 0, 1)
        for h0 in range(0, H, 2):
            pair(slot, least, k, h0)
            if h0 == 0:
                between()

    def part_copies(kind):
        res = []
        if kind == SIDE:
            res.append(remote(part.at[kind, y], rx.at[kind, 0],
                              p_send.at[kind, 0], p_recv.at[kind, 0], (at(2), y)))
        to = at(2) if kind == SIDE else me
        res.append(remote(part.at[kind, 1 - y], rx.at[kind, 1],
                          p_send.at[kind, 1], p_recv.at[kind, 1], (to, 1 - y)))
        return res

    def send_part(kind):
        for copy in part_copies(kind):
            copy.start()

    def give(p):
        return remote(acc.at[2 * p + 1 + c], take.at[p], d_send.at[p], d_recv.at[p], (at(1), y))

    def join(p):
        give(p).wait_recv()
        part[NEAR + p] = (acc[2 * p + 2 - c] + take[p]).astype(BF16)
        send_part(NEAR + p)

    z_copies = [
        remote(zs.at[m], fin.at[m], z_send.at[m], z_recv.at[m], (to, y))
        for m, to in enumerate((plane(-1), owner(2), owner(1)))
    ]

    def forward(m, *kinds):
        total = arrived_part(kinds[0])
        for kind in kinds[1:]:
            total = total + arrived_part(kind)
        zs[m] = total.astype(BF16)
        z_copies[m].start()

    def arrived_part(kind):
        def get(m):
            remote(rx.at[kind, m], rx.at[kind, m], p_send.at[0, 0], p_recv.at[kind, m],
                   (at(1), y)).wait_recv()
            return rx[kind, m].astype(F32)

        first = part[kind, y].astype(F32) if kind != SIDE else get(0)
        return first + get(1)

    i_odd, i_even = 2 * x + 1, 2 * x
    o_odd, o_even = 3 - 2 * x, 2 - 2 * x

    def step0():
        on(0, up_b.start)
        on(1, side_own)

    compute(A(j), 0, j, 0, step0)
    part[OWN] = acc[0].astype(BF16)

    on(1, spread_b)
    on(0, lambda: kv_arrived(B(mate(1))))

    def step1():
        send_part(OWN)
        on(0, spread_b)

    compute(B(i_odd), 1, i_odd, 1, step1)
    on(0, give(0).start)
    on(1, lambda: kv_arrived(B(mate(1))))

    def step2():
        on(1, relay_b, lambda: join(0), pass_c)

    compute(B(i_even), 1, i_even, 2, step2)
    on(1, give(0).start)
    on(0, lambda: kv_arrived(B(mate(3))))

    def step3():
        on(0, relay_b, lambda: join(0), pass_c)

    compute(B(o_odd), 1, o_odd, 3, step3)
    on(0, give(1).start)
    on(1, lambda: kv_arrived(B(mate(3))))

    def step4():
        on(1, lambda: join(1), relay_a)

    compute(B(o_even), 1, o_even, 4, step4)
    on(1, give(1).start)
    on(0, lambda: kv_arrived(A(mate(3))))

    def step5():
        on(0, lambda: join(1))

    compute(A(o_odd), 0, o_odd, 5, step5)
    on(0, give(2).start)
    kv_arrived(A(mate(1)))

    def step6():
        on(1, lambda: join(2))
        on(0, relay_a)

    compute(A(mate(1)), 0, mate(1), 7, step6)
    part[MATE] = acc[7].astype(BF16)
    send_part(MATE)
    on(1, lambda: kv_arrived(A(mate(3))))

    def step7():
        pass

    compute(A(o_even), 0, o_even, 6, step7)
    on(1, give(2).start)
    forward(0, NEAR, SIDE)
    on(1, lambda: forward(1, FAR))
    on(0, lambda: join(2))
    forward(2, MATE)

    for h in range(H):
        dq[:, h * D:(h + 1) * D] = dqt[h].astype(BF16)
    dq_copy = pltpu.make_async_copy(dq, dq_out, out_sem)
    dq_copy.start()
    on(0, lambda: forward(1, FAR))

    mine = arrived_part(OWN)
    for copy, m in zip(z_copies, range(3)):
        copy.wait_recv()
        mine = mine + fin[m].astype(F32)
    dk_out[...] = mine[:D].T.astype(BF16)
    dv_out[...] = mine[D:].T.astype(BF16)

    for copy in [up_b, own[1], own[2], b_out[1], b_out[2], b_relay, a_relay]:
        copy.wait_send()
    pl.when(j > 0)(up_c.wait_send)
    for kind in range(5):
        for copy in part_copies(kind):
            copy.wait_send()
    for p in range(PAIRS):
        give(p).wait_send()
    for copy in z_copies:
        copy.wait_send()
    dq_copy.wait()


def shards(n, query, key_rows, value_rows, output, grad_output, log_norm, stripe):
    S, W = query.shape
    D = key_rows.shape[1]
    H = W // D
    half = S // 2
    any_ = pl.BlockSpec(memory_space=pl.ANY)
    vm = pl.BlockSpec(memory_space=pltpu.VMEM)
    dma = pltpu.SemaphoreType.DMA
    return pl.pallas_call(
        functools.partial(kernel, n),
        out_shape=(
            jax.ShapeDtypeStruct((S, W), BF16),
            jax.ShapeDtypeStruct((half, D), BF16),
            jax.ShapeDtypeStruct((half, D), BF16),
        ),
        in_specs=[pl.BlockSpec(memory_space=pltpu.SMEM)] + [any_] * 6,
        out_specs=(any_, vm, vm),
        scratch_shapes=[
            pltpu.VMEM((S, W), BF16),
            pltpu.VMEM((S, W), BF16),
            pltpu.VMEM((S, W), BF16),
            pltpu.VMEM((H, S), F32),
            pltpu.VMEM((H, S, D), F32),
            pltpu.VMEM((H, S, D), F32),
            pltpu.VMEM((H, D, S), BF16),
            pltpu.VMEM((H, D, S), BF16),
            pltpu.VMEM((2 * GROUP + 1, S, 2 * D), BF16),
            pltpu.VMEM((H, S, D), F32),
            pltpu.VMEM((WINDOW, 2, 2 * D, half), F32),
            pltpu.VMEM((PAIRS, 2, 2 * D, half), F32),
            pltpu.VMEM((5, 2, 2 * D, half), BF16),
            pltpu.VMEM((5, 2, 2 * D, half), BF16),
            pltpu.VMEM((3, 2 * D, half), BF16),
            pltpu.VMEM((3, 2 * D, half), BF16),
            pltpu.VMEM((S, W), BF16),
            dma((6,)),
            dma(()),
            dma((8,)),
            dma((2 * GROUP + 1,)),
            dma((PAIRS,)),
            dma((PAIRS,)),
            dma((5, 2)),
            dma((5, 2)),
            dma((3,)),
            dma((3,)),
        ],
        compiler_params=pltpu.CompilerParams(
            collective_id=0, has_side_effects=True, vmem_limit_bytes=67043328
        ),
        name="window_backward",
    )(stripe, query, key_rows, value_rows, output, grad_output, log_norm)


def solution(mesh):
    placed = (
        P("seq", "head"),
        P("seq", None),
        P("seq", None),
        P("seq", "head"),
        P("seq", "head"),
        P("head", "seq"),
        P(),
    )
    return jax.shard_map(
        functools.partial(shards, mesh.shape["seq"]),
        mesh=mesh,
        in_specs=placed,
        out_specs=(P("seq", "head"), P(("seq", "head"), None), P(("seq", "head"), None)),
        check_vma=False,
    )
```

time: 60.7 us -> 49.6 us (0.82)
  the two profiles are of different devices: /device:TPU:0 before, /device:TPU:2 now
where the time goes in v1:
time: 49.6 us; the launch traced here: 49.1 us
  Pallas kernels  45.1 us (91%)
  local copies, waits for them, and re-layouts  3.4 us (7%)
  between operations  0.65 us (1%)
    pallas_call x1, Pallas kernels, shards(): pl.pallas_call(functools.partial(kernel, n), out_shape=(jax.ShapeDtypeStr...  45.1 us
    unnamed x7, local copies, waits for them, and re-layouts  3.4 us

profile of v1, /device:TPU:2, one launch (start us, length us, event | category | flops | bytes accessed | tf_op | source)
XLA Modules:
  0.0 49.1 jit_solution(459875288473878050)
XLA Ops:
  0.6 45.1 %window_backward.1 = (bf16[512,512]{1,0:T(8,128)(2,1)}, bf16[256,128]{1,0:T(8,128)(2,1)}, bf16[256,128]{1,0:T(8,128)(2,1)}) custom-call(s32[16]{0:T(128)} %stripe.1, bf16[512,512]{1,0:T(8,128)(2,1)} %q_hbm.1, bf16[512,128]{1,0:T(8,128)(2,1)} %k_hbm.1, bf16[512,128]{1,0:T(8,128)(2,1)} %v_hbm.1, bf16[512,512]{1,0:T(8,128)(2,1)} %o_hbm.1, ...), custom_call_target="tpu_custom_call" | custom-call | tf_op jit(solution)/shard_map/window_backward/pallas_call | solution.py:362
  45.7 0.0 copy-start.1
  45.7 1.9 %copy.13 = bf16[512,512]{1,0:T(8,128)(2,1)} copy(bf16[512,512]{1,0:T(8,128)(2,1)} %get-tuple-element.6) | data formatting | bytes 1048576
  47.6 0.0 copy-done.1
  47.6 0.0 copy-start
  47.6 0.6 %copy.14 = bf16[256,128]{1,0:T(8,128)(2,1)} copy(bf16[256,128]{1,0:T(8,128)(2,1)S(1)} %copy-done.1) | data formatting | bytes 131072
  48.3 0.2 copy-done
  48.5 0.6 %copy.15 = bf16[256,128]{1,0:T(8,128)(2,1)} copy(bf16[256,128]{1,0:T(8,128)(2,1)S(1)} %copy-done) | data formatting | bytes 131072
Async XLA Ops:
  45.7 1.9 %copy-start.1 = (bf16[256,128]{1,0:T(8,128)(2,1)S(1)}, bf16[256,128]{1,0:T(8,128)(2,1)}, u32[]{:S(2)}) copy-start(bf16[256,128]{1,0:T(8,128)(2,1)} %get-tuple-element.7) | copy-start | bytes 196612
  47.6 0.9 %copy-start = (bf16[256,128]{1,0:T(8,128)(2,1)S(1)}, bf16[256,128]{1,0:T(8,128)(2,1)}, u32[]{:S(2)}) copy-start(bf16[256,128]{1,0:T(8,128)(2,1)} %get-tuple-element.8) | copy-start | bytes 196612

commit v2 on v1

--- a/solution.py
+++ b/solution.py
@@ -23,10 +23,10 @@
 
 
 def kernel(
-    n, stripe, q_hbm, k_hbm, v_hbm, o_hbm, g_hbm, lse_hbm,
+    n, stripe_hbm, q_hbm, k_hbm, v_hbm, o_hbm, g_hbm, lse_hbm,
     dq_out, dk_out, dv_out,
-    q, g, o, lse, delta, level, qt, gt, kv, dqt, acc, take, part, rx, zs, fin, dq,
-    in_sem, out_sem, kv_send, kv_recv, d_send, d_recv, p_send, p_recv, z_send, z_recv,
+    stripe, q, g, o, lse, delta, level, qt, gt, kv, dqt, acc, lend, take, part, rx, zs, fin,
+    in_sem, kv_send, kv_recv, d_send, d_recv, p_send, p_recv, z_send, z_recv,
 ):
     me = lax.axis_index("seq")
     y = lax.axis_index("head")
@@ -60,6 +60,7 @@
         pltpu.make_async_copy(g_hbm, g, in_sem.at[3]),
         pltpu.make_async_copy(o_hbm, o, in_sem.at[4]),
         pltpu.make_async_copy(lse_hbm, lse, in_sem.at[5]),
+        pltpu.make_async_copy(stripe_hbm, stripe, in_sem.at[6]),
     ]
     for load in loads:
         load.start()
@@ -78,7 +79,68 @@
     peers += [(partner(t), y) for t in (1, 2)]
     for p in peers:
         pl.semaphore_signal(barrier, inc=1, device_id=p, device_id_type=pl.DeviceIdType.MESH)
-    for load in loads:
+    loads[0].wait()
+    loads[1].wait()
+    pl.semaphore_wait(barrier, len(peers))
+
+    A = lambda i: i
+    B = lambda i: GROUP + i
+    C = 2 * GROUP
+
+    def remote(src, dst, ss, rs, to):
+        return pltpu.make_async_remote_copy(
+            src_ref=src, dst_ref=dst, send_sem=ss, recv_sem=rs,
+            device_id=to, device_id_type=pl.DeviceIdType.MESH,
+        )
+
+    def kv_copy(src, dst, sem, to):
+        return remote(kv.at[src], kv.at[dst], kv_send.at[sem], kv_recv.at[dst], (to, y))
+
+    up_b = kv_copy(A(j), B(j), 0, plane(1))
+    up_c = kv_copy(B(j), C, 1, plane(1))
+    own = {t: kv_copy(A(j), A(j), 1 + t, at(t)) for t in (1, 2)}
+    late = {t: kv_copy(C, A(j), 1 + t, at(t)) for t in (1, 2)}
+    b_out = {t: kv_copy(B(j), B(j), 3 + t, at(t)) for t in (1, 2)}
+    b_relay = kv_copy(B(mate(2)), B(mate(2)), 6, at(1))
+    a_relay = kv_copy(A(mate(2)), A(mate(2)), 7, at(1))
+
+    def kv_arrived(slot):
+        kv_copy(slot, slot, 0, at(1)).wait_recv()
+
+    def on(core, *acts):
+        @pl.when(c == core)
+        def _():
+            for act in acts:
+                act()
+
+    def spread_b():
+        kv_arrived(B(j))
+        b_out[1].start()
+        b_out[2].start()
+        pl.when(j > 0)(up_c.start)
+
+    def relay_b():
+        kv_arrived(B(mate(2)))
+        b_relay.start()
+
+    def relay_a():
+        kv_arrived(A(mate(2)))
+        a_relay.start()
+
+    def pass_c():
+        @pl.when(j > 0)
+        def _():
+            kv_arrived(C)
+            pl.when(x == 1)(late[2].start)
+            pl.when(c == 1)(late[1].start)
+
+    def side_own():
+        pl.when(x == 0)(own[2].start)
+
+    on(1, up_b.start)
+    on(0, own[1].start, side_own)
+
+    for load in loads[2:]:
         load.wait()
 
     for h in range(H):
@@ -90,65 +152,6 @@
         level[h] = line.T
         qt[h] = q[:, cols].T
         gt[h] = g[:, cols].T
-    pl.semaphore_wait(barrier, len(peers))
-
-    A = lambda i: i
-    B = lambda i: GROUP + i
-    C = 2 * GROUP
-
-    def remote(src, dst, ss, rs, to):
-        return pltpu.make_async_remote_copy(
-            src_ref=src, dst_ref=dst, send_sem=ss, recv_sem=rs,
-            device_id=to, device_id_type=pl.DeviceIdType.MESH,
-        )
-
-    def kv_copy(src, dst, sem, to):
-        return remote(kv.at[src], kv.at[dst], kv_send.at[sem], kv_recv.at[dst], (to, y))
-
-    up_b = kv_copy(A(j), B(j), 0, plane(1))
-    up_c = kv_copy(B(j), C, 1, plane(1))
-    own = {t: kv_copy(A(j), A(j), 1 + t, at(t)) for t in (1, 2)}
-    late = {t: kv_copy(C, A(j), 1 + t, at(t)) for t in (1, 2)}
-    b_out = {t: kv_copy(B(j), B(j), 3 + t, at(t)) for t in (1, 2)}
-    b_relay = kv_copy(B(mate(2)), B(mate(2)), 6, at(1))
-    a_relay = kv_copy(A(mate(2)), A(mate(2)), 7, at(1))
-
-    def kv_arrived(slot):
-        kv_copy(slot, slot, 0, at(1)).wait_recv()
-
-    def on(core, *acts):
-        @pl.when(c == core)
-        def _():
-            for act in acts:
-                act()
-
-    def spread_b():
-        kv_arrived(B(j))
-        b_out[1].start()
-        b_out[2].start()
-        pl.when(j > 0)(up_c.start)
-
-    def relay_b():
-        kv_arrived(B(mate(2)))
-        b_relay.start()
-
-    def relay_a():
-        kv_arrived(A(mate(2)))
-        a_relay.start()
-
-    def pass_c():
-        @pl.when(j > 0)
-        def _():
-            kv_arrived(C)
-            pl.when(x == 1)(late[2].start)
-            pl.when(c == 1)(late[1].start)
-
-    def side_own():
-        pl.when(x == 0)(own[2].start)
-
-    on(1, up_b.start)
-    on(0, own[1].start, side_own)
-
     dqt[...] = jnp.zeros_like(dqt)
     own_stripe = stripe[me]
 
@@ -229,11 +232,15 @@
             copy.start()
 
     def give(p):
-        return remote(acc.at[2 * p + 1 + c], take.at[p], d_send.at[p], d_recv.at[p], (at(1), y))
+        return remote(lend.at[p], take.at[p], d_send.at[p], d_recv.at[p], (at(1), y))
+
+    def lend_out(p):
+        lend[p] = acc[2 * p + 1 + c].astype(BF16)
+        give(p).start()
 
     def join(p):
         give(p).wait_recv()
-        part[NEAR + p] = (acc[2 * p + 2 - c] + take[p]).astype(BF16)
+        part[NEAR + p] = (acc[2 * p + 2 - c] + take[p].astype(F32)).astype(BF16)
         send_part(NEAR + p)
 
     z_copies = [
@@ -260,13 +267,11 @@
     i_odd, i_even = 2 * x + 1, 2 * x
     o_odd, o_even = 3 - 2 * x, 2 - 2 * x
 
-    def step0():
-        on(0, up_b.start)
-        on(1, side_own)
-
-    compute(A(j), 0, j, 0, step0)
+    on(0, up_b.start)
+    on(1, side_own)
+
+    compute(A(j), 0, j, 0, lambda: None)
     part[OWN] = acc[0].astype(BF16)
-
     on(1, spread_b)
     on(0, lambda: kv_arrived(B(mate(1))))
 
@@ -275,61 +280,58 @@
         on(0, spread_b)
 
     compute(B(i_odd), 1, i_odd, 1, step1)
-    on(0, give(0).start)
+    on(0, lambda: lend_out(0))
     on(1, lambda: kv_arrived(B(mate(1))))
 
     def step2():
         on(1, relay_b, lambda: join(0), pass_c)
 
     compute(B(i_even), 1, i_even, 2, step2)
-    on(1, give(0).start)
-    on(0, lambda: kv_arrived(B(mate(3))))
+    on(1, lambda: lend_out(0))
+    kv_arrived(A(mate(1)))
 
     def step3():
         on(0, relay_b, lambda: join(0), pass_c)
 
-    compute(B(o_odd), 1, o_odd, 3, step3)
-    on(0, give(1).start)
+    compute(A(mate(1)), 0, mate(1), 7, step3)
+    part[MATE] = acc[7].astype(BF16)
+    on(0, lambda: kv_arrived(B(mate(3))))
+
+    def step4():
+        send_part(MATE)
+        on(1, relay_a)
+
+    compute(B(o_odd), 1, o_odd, 3, step4)
+    on(0, lambda: lend_out(1))
     on(1, lambda: kv_arrived(B(mate(3))))
 
-    def step4():
-        on(1, lambda: join(1), relay_a)
-
-    compute(B(o_even), 1, o_even, 4, step4)
-    on(1, give(1).start)
+    def step5():
+        on(1, lambda: join(1))
+        on(0, relay_a)
+
+    compute(B(o_even), 1, o_even, 4, step5)
+    on(1, lambda: lend_out(1))
     on(0, lambda: kv_arrived(A(mate(3))))
 
-    def step5():
+    def step6():
         on(0, lambda: join(1))
-
-    compute(A(o_odd), 0, o_odd, 5, step5)
-    on(0, give(2).start)
-    kv_arrived(A(mate(1)))
-
-    def step6():
+        forward(2, MATE)
+
+    compute(A(o_odd), 0, o_odd, 5, step6)
+    on(0, lambda: lend_out(2))
+    on(1, lambda: kv_arrived(A(mate(3))))
+
+    def step7():
         on(1, lambda: join(2))
-        on(0, relay_a)
-
-    compute(A(mate(1)), 0, mate(1), 7, step6)
-    part[MATE] = acc[7].astype(BF16)
-    send_part(MATE)
-    on(1, lambda: kv_arrived(A(mate(3))))
-
-    def step7():
-        pass
 
     compute(A(o_even), 0, o_even, 6, step7)
-    on(1, give(2).start)
+    on(1, lambda: lend_out(2))
+
+    for h in range(H):
+        dq_out[:, h * D:(h + 1) * D] = dqt[h].astype(BF16)
+    on(0, lambda: join(2))
     forward(0, NEAR, SIDE)
-    on(1, lambda: forward(1, FAR))
-    on(0, lambda: join(2))
-    forward(2, MATE)
-
-    for h in range(H):
-        dq[:, h * D:(h + 1) * D] = dqt[h].astype(BF16)
-    dq_copy = pltpu.make_async_copy(dq, dq_out, out_sem)
-    dq_copy.start()
-    on(0, lambda: forward(1, FAR))
+    forward(1, FAR)
 
     mine = arrived_part(OWN)
     for copy, m in zip(z_copies, range(3)):
@@ -348,7 +350,14 @@
         give(p).wait_send()
     for copy in z_copies:
         copy.wait_send()
-    dq_copy.wait()
+
+
+def emit(*refs):
+    copies = [pltpu.make_async_copy(refs[m], refs[3 + m], refs[6].at[m]) for m in range(3)]
+    for copy in copies:
+        copy.start()
+    for copy in copies:
+        copy.wait()
 
 
 def shards(n, query, key_rows, value_rows, output, grad_output, log_norm, stripe):
@@ -359,16 +368,18 @@
     any_ = pl.BlockSpec(memory_space=pl.ANY)
     vm = pl.BlockSpec(memory_space=pltpu.VMEM)
     dma = pltpu.SemaphoreType.DMA
-    return pl.pallas_call(
+    arrays = (stripe, query, key_rows, value_rows, output, grad_output, log_norm)
+    found = pl.pallas_call(
         functools.partial(kernel, n),
         out_shape=(
             jax.ShapeDtypeStruct((S, W), BF16),
             jax.ShapeDtypeStruct((half, D), BF16),
             jax.ShapeDtypeStruct((half, D), BF16),
         ),
-        in_specs=[pl.BlockSpec(memory_space=pltpu.SMEM)] + [any_] * 6,
-        out_specs=(any_, vm, vm),
+        in_specs=[pl.BlockSpec(memory_space=pltpu.HBM)] * 7,
+        out_specs=(vm, vm, vm),
         scratch_shapes=[
+            pltpu.SMEM(stripe.shape, jnp.int32),
             pltpu.VMEM((S, W), BF16),
             pltpu.VMEM((S, W), BF16),
             pltpu.VMEM((S, W), BF16),
@@ -380,14 +391,13 @@
             pltpu.VMEM((2 * GROUP + 1, S, 2 * D), BF16),
             pltpu.VMEM((H, S, D), F32),
             pltpu.VMEM((WINDOW, 2, 2 * D, half), F32),
-            pltpu.VMEM((PAIRS, 2, 2 * D, half), F32),
+            pltpu.VMEM((PAIRS, 2, 2 * D, half), BF16),
+            pltpu.VMEM((PAIRS, 2, 2 * D, half), BF16),
             pltpu.VMEM((5, 2, 2 * D, half), BF16),
             pltpu.VMEM((5, 2, 2 * D, half), BF16),
             pltpu.VMEM((3, 2 * D, half), BF16),
             pltpu.VMEM((3, 2 * D, half), BF16),
-            pltpu.VMEM((S, W), BF16),
-            dma((6,)),
-            dma(()),
+            dma((7,)),
             dma((8,)),
             dma((2 * GROUP + 1,)),
             dma((PAIRS,)),
@@ -398,10 +408,19 @@
             dma((3,)),
         ],
         compiler_params=pltpu.CompilerParams(
-            collective_id=0, has_side_effects=True, vmem_limit_bytes=67043328
+            collective_id=0, has_side_effects=True, vmem_limit_bytes=33554432
         ),
         name="window_backward",
-    )(stripe, query, key_rows, value_rows, output, grad_output, log_norm)
+    )(*(pltpu.with_memory_space_constraint(a, pltpu.HBM) for a in arrays))
+    return pl.pallas_call(
+        emit,
+        out_shape=tuple(jax.ShapeDtypeStruct(a.shape, a.dtype) for a in found),
+        in_specs=[vm] * 3,
+        out_specs=(any_,) * 3,
+        scratch_shapes=[dma((3,))],
+        compiler_params=pltpu.CompilerParams(vmem_limit_bytes=1 << 22),
+        name="emit",
+    )(*found)
 
 
 def solution(mesh):

time: 49.6 us -> 43.7 us (0.88)
  local copies, waits for them, and re-layouts: 3.4 us -> 0 us
  Pallas kernels: 45.1 us -> 42.7 us
    unnamed x7 -> x0, local copies, waits for them, and re-layouts: 3.4 us -> none
    pallas_call x1, Pallas kernels: 45.1 us -> 41.9 us  [shards(): pl.pallas_call(functools.partial(kernel, n), out_shape=(jax.ShapeDtypeStr...]
    pallas_call x0 -> x1, Pallas kernels: none -> 0.85 us  [shards(): pl.pallas_call(emit, out_shape=tuple((jax.ShapeDtypeStruct(a.shape, a.dty...]
where the time goes in v2:
time: 43.7 us; the launch traced here: 43.5 us
  Pallas kernels  42.7 us (98%)
  between operations  0.8 us (2%)
    pallas_call x1, Pallas kernels, shards(): pl.pallas_call(functools.partial(kernel, n), out_shape=(jax.ShapeDtypeStr...  41.9 us

profile of v2, /device:TPU:2, one launch (start us, length us, event | category | flops | bytes accessed | tf_op | source)
XLA Modules:
  0.0 43.5 jit_solution(80030360992253046)
XLA Ops:
  0.6 41.9 %window_backward.1 = (bf16[512,512]{1,0:T(8,128)(2,1)S(1)}, bf16[256,128]{1,0:T(8,128)(2,1)S(1)}, bf16[256,128]{1,0:T(8,128)(2,1)S(1)}) custom-call(s32[16]{0:T(128)} %stripe_hbm.1, bf16[512,512]{1,0:T(8,128)(2,1)} %q_hbm.1, bf16[512,128]{1,0:T(8,128)(2,1)} %k_hbm.1, bf16[512,128]{1,0:T(8,128)(2,1)} %v_hbm.1, bf16[512,512]{1,0:T(8,128)(2,1)} %o_hbm.1, ...), custom_call_target="tpu_custom_call" | custom-call | tf_op jit(solution)/shard_map/window_backward/pallas_call | solution.py:372
  42.5 0.9 %emit.1 = (bf16[512,512]{1,0:T(8,128)(2,1)}, bf16[256,128]{1,0:T(8,128)(2,1)}, bf16[256,128]{1,0:T(8,128)(2,1)}) custom-call(bf16[512,512]{1,0:T(8,128)(2,1)S(1)} %get-tuple-element.6.refs_0_, bf16[256,128]{1,0:T(8,128)(2,1)S(1)} %get-tuple-element.7.refs_1_, bf16[256,128]{1,0:T(8,128)(2,1)S(1)} %get-tuple-element.8.refs_2_), custom_call_target="tpu_custom_call" | custom-call | tf_op jit(solution)/shard_map/emit/pallas_call | solution.py:415

commit v3 on v2

--- a/solution.py
+++ b/solution.py
@@ -205,11 +205,14 @@
                     total = total + acc[k, w, m * D:(m + 1) * D, :]
                 acc[k, w, m * D:(m + 1) * D, :] = total
 
-    def compute(slot, late_flag, i, k, between):
-        if late_flag:
-            source = base - GROUP + i
-        else:
-            source = base + i - jnp.where(i > j, 2 * GROUP, 0)
+    def near(i):
+        return B(i), base - GROUP + i
+
+    def side(i):
+        return A(i), base + i - jnp.where(i > j, 2 * GROUP, 0)
+
+    def compute(block, k, between):
+        slot, source = block
         source = lax.rem(source + n, n)
         least = jnp.where(stripe[source] <= own_stripe, 0, 1)
         for h0 in range(0, H, 2):
@@ -270,66 +273,66 @@
     on(0, up_b.start)
     on(1, side_own)
 
-    compute(A(j), 0, j, 0, lambda: None)
+    def either(at0, at1):
+        return (1 - c) * at0 + c * at1
+
+    compute(side(j), 0, lambda: None)
     part[OWN] = acc[0].astype(BF16)
-    on(1, spread_b)
+    on(1, spread_b, lambda: kv_arrived(A(mate(1))))
     on(0, lambda: kv_arrived(B(mate(1))))
 
     def step1():
         send_part(OWN)
         on(0, spread_b)
 
-    compute(B(i_odd), 1, i_odd, 1, step1)
+    compute(near(i_odd), 1, step1)
     on(0, lambda: lend_out(0))
-    on(1, lambda: kv_arrived(B(mate(1))))
-
-    def step2():
-        on(1, relay_b, lambda: join(0), pass_c)
-
-    compute(B(i_even), 1, i_even, 2, step2)
-    on(1, lambda: lend_out(0))
-    kv_arrived(A(mate(1)))
+
+    even, own_side = near(i_even), side(mate(1))
+    compute(tuple(map(either, even, own_side)), either(2, 7), lambda: None)
+    on(0, lambda: kv_arrived(A(mate(1))))
+    on(1, pass_c, lambda: kv_arrived(B(mate(1))))
 
     def step3():
-        on(0, relay_b, lambda: join(0), pass_c)
-
-    compute(A(mate(1)), 0, mate(1), 7, step3)
+        on(0, pass_c)
+        on(1, lambda: join(0))
+
+    compute(tuple(map(either, own_side, even)), either(7, 2), step3)
     part[MATE] = acc[7].astype(BF16)
     on(0, lambda: kv_arrived(B(mate(3))))
+    on(1, lambda: lend_out(0), relay_b)
 
     def step4():
         send_part(MATE)
-        on(1, relay_a)
-
-    compute(B(o_odd), 1, o_odd, 3, step4)
+        on(0, relay_b, lambda: join(0))
+
+    compute(near(o_odd), 3, step4)
     on(0, lambda: lend_out(1))
     on(1, lambda: kv_arrived(B(mate(3))))
 
     def step5():
-        on(1, lambda: join(1))
-        on(0, relay_a)
-
-    compute(B(o_even), 1, o_even, 4, step5)
+        on(1, relay_a, lambda: join(1))
+
+    compute(near(o_even), 4, step5)
     on(1, lambda: lend_out(1))
     on(0, lambda: kv_arrived(A(mate(3))))
 
     def step6():
-        on(0, lambda: join(1))
-        forward(2, MATE)
-
-    compute(A(o_odd), 0, o_odd, 5, step6)
+        on(0, relay_a, lambda: join(1))
+
+    compute(side(o_odd), 5, step6)
     on(0, lambda: lend_out(2))
     on(1, lambda: kv_arrived(A(mate(3))))
 
     def step7():
-        on(1, lambda: join(2))
-
-    compute(A(o_even), 0, o_even, 6, step7)
+        forward(2, MATE)
+
+    compute(side(o_even), 6, step7)
     on(1, lambda: lend_out(2))
 
     for h in range(H):
         dq_out[:, h * D:(h + 1) * D] = dqt[h].astype(BF16)
-    on(0, lambda: join(2))
+    join(2)
     forward(0, NEAR, SIDE)
     forward(1, FAR)
 

time: 43.7 us -> 43.2 us (0.989)
  no operation moved by 1% of the time
where the time goes in v3:
time: 43.2 us; the launch traced here: 43.1 us
  Pallas kernels  42.3 us (98%)
  between operations  0.8 us (2%)
    pallas_call x1, Pallas kernels, shards(): pl.pallas_call(functools.partial(kernel, n), out_shape=(jax.ShapeDtypeStr...  41.4 us

profile of v3, /device:TPU:2, one launch (start us, length us, event | category | flops | bytes accessed | tf_op | source)
XLA Modules:
  0.0 43.1 jit_solution(12328670053281331355)
XLA Ops:
  0.6 41.4 %window_backward.1 = (bf16[512,512]{1,0:T(8,128)(2,1)S(1)}, bf16[256,128]{1,0:T(8,128)(2,1)S(1)}, bf16[256,128]{1,0:T(8,128)(2,1)S(1)}) custom-call(s32[16]{0:T(128)} %stripe_hbm.1, bf16[512,512]{1,0:T(8,128)(2,1)} %q_hbm.1, bf16[512,128]{1,0:T(8,128)(2,1)} %k_hbm.1, bf16[512,128]{1,0:T(8,128)(2,1)} %v_hbm.1, bf16[512,512]{1,0:T(8,128)(2,1)} %o_hbm.1, ...), custom_call_target="tpu_custom_call" | custom-call | tf_op jit(solution)/shard_map/window_backward/pallas_call | solution.py:375
  42.1 0.9 %emit.1 = (bf16[512,512]{1,0:T(8,128)(2,1)}, bf16[256,128]{1,0:T(8,128)(2,1)}, bf16[256,128]{1,0:T(8,128)(2,1)}) custom-call(bf16[512,512]{1,0:T(8,128)(2,1)S(1)} %get-tuple-element.6.refs_0_, bf16[256,128]{1,0:T(8,128)(2,1)S(1)} %get-tuple-element.7.refs_1_, bf16[256,128]{1,0:T(8,128)(2,1)S(1)} %get-tuple-element.8.refs_2_), custom_call_target="tpu_custom_call" | custom-call | tf_op jit(solution)/shard_map/emit/pallas_call | solution.py:418

commit v4 on v3

--- a/solution.py
+++ b/solution.py
@@ -14,7 +14,7 @@
 BF16 = jnp.bfloat16
 OWN, NEAR, SIDE, FAR, MATE = range(5)
 PAIRS = 3
-QUADS = ((1, 1), (1, 0), (0, 0))
+QUADS = ((0, 0), (1, 0), (1, 1))
 LAG = 3
 
 
@@ -188,7 +188,7 @@
             add(dv, w, dot(gt[h, :, rows(r)], p.astype(BF16), 1, 0))
             add(dk, w, dot(qt[h, :, rows(r)], d, 1, 0))
             add(dq_part, (h, r), dot(d, ks[w], 1, 0))
-            if w == 0:
+            if r == w:
                 dqt[h, rows(r)] += dq_part[h, r]
 
         waiting = []
@@ -325,6 +325,7 @@
     on(1, lambda: kv_arrived(A(mate(3))))
 
     def step7():
+        on(1, lambda: join(2))
         forward(2, MATE)
 
     compute(side(o_even), 6, step7)
@@ -332,7 +333,7 @@
 
     for h in range(H):
         dq_out[:, h * D:(h + 1) * D] = dqt[h].astype(BF16)
-    join(2)
+    on(0, lambda: join(2))
     forward(0, NEAR, SIDE)
     forward(1, FAR)
 

time: 43.2 us -> 43.2 us (level)
  no operation moved by 1% of the time
where the time goes in v4:
time: 43.2 us; the launch traced here: 43.1 us
  Pallas kernels  42.3 us (98%)
  between operations  0.8 us (2%)
    pallas_call x1, Pallas kernels, shards(): pl.pallas_call(functools.partial(kernel, n), out_shape=(jax.ShapeDtypeStr...  41.4 us

profile of v4, /device:TPU:2, one launch (start us, length us, event | category | flops | bytes accessed | tf_op | source)
XLA Modules:
  0.0 43.1 jit_solution(7546905724226192931)
XLA Ops:
  0.6 41.4 %window_backward.1 = (bf16[512,512]{1,0:T(8,128)(2,1)S(1)}, bf16[256,128]{1,0:T(8,128)(2,1)S(1)}, bf16[256,128]{1,0:T(8,128)(2,1)S(1)}) custom-call(s32[16]{0:T(128)} %stripe_hbm.1, bf16[512,512]{1,0:T(8,128)(2,1)} %q_hbm.1, bf16[512,128]{1,0:T(8,128)(2,1)} %k_hbm.1, bf16[512,128]{1,0:T(8,128)(2,1)} %v_hbm.1, bf16[512,512]{1,0:T(8,128)(2,1)} %o_hbm.1, ...), custom_call_target="tpu_custom_call" | custom-call | tf_op jit(solution)/shard_map/window_backward/pallas_call | solution.py:376
  42.0 0.9 %emit.1 = (bf16[512,512]{1,0:T(8,128)(2,1)}, bf16[256,128]{1,0:T(8,128)(2,1)}, bf16[256,128]{1,0:T(8,128)(2,1)}) custom-call(bf16[512,512]{1,0:T(8,128)(2,1)S(1)} %get-tuple-element.6.refs_0_, bf16[256,128]{1,0:T(8,128)(2,1)S(1)} %get-tuple-element.7.refs_1_, bf16[256,128]{1,0:T(8,128)(2,1)S(1)} %get-tuple-element.8.refs_2_), custom_call_target="tpu_custom_call" | custom-call | tf_op jit(solution)/shard_map/emit/pallas_call | solution.py:419
